TPU v7x, 256 devices: a whole 4x4x8 slice. The times are simulated.
256 devices in a mesh: fsdp: 16 (over y, z_lo, core), sp: 16 (over x, z_hi).
Axes of the slice: x: 4, y: 4, z: 8 (z_hi: 4, z_lo: 2; z = z_hi * 2 + z_lo), core: 2. Of those that a mesh axis runs over, the one named last changes fastest.
Arguments:
- hidden: bfloat16 [16, 4096, 5120], P('fsdp', 'sp'), may hold values from -6 to 6
- queries: bfloat16 [16, 4096, 4096], P('fsdp', 'sp'), may hold values from -240 to 240
- norm_gain: float32 [5120], replicated, may hold values from 0.5 to 1.5
- kv_weight: bfloat16 [5120, 2048], P('fsdp'), may hold values from -0.078125 to 0.078125
- value_bias: float32 [1024], replicated, may hold values from -3 to 3
- doc_lengths: int32 [16, 16], P('fsdp'), may hold values from 1 to 1024, 4096 in all within a row
Outputs:
- attended: bfloat16 [16, 4096, 4096], P('fsdp', 'sp')
Inputs may be any that keep to these rules, and one draw needn't show every extreme that they name: `doc_lengths`: each row sums to 4096 and its largest entry is 1024.
All inputs are finite; a program needn't handle non-finite values.
Results may differ from a plain program's by a relative error of at most 0.0067.
Values may be sent and summed in bfloat16 or wider, within the bound.
A program may use at most 128 MiB of HBM per device.

v0:
```python
import jax
import jax.numpy as jnp
from jax import lax
from jax.sharding import PartitionSpec as P

QH = 32
KVH = 8
HD = 128


EPS = 1e-06


def from_behind(value, axis, by):
    count = lax.axis_size(axis)
    pairs = [(i, i + by) for i in range(count) if 0 <= i + by < count]
    return lax.ppermute(value, axis, pairs)


def attend_near(query_rows, key_all, value_all, query_pos, key_pos, query_ids, key_ids):
    token_count = query_rows.shape[0]
    ratio = QH // KVH
    scale = HD ** (-0.5)
    allowed = (
        (key_pos[None, :] >= 0)
        & (key_pos[None, :] <= query_pos[:, None])
        & (key_ids[None, :] == query_ids[:, None])
    )
    query_groups = jnp.transpose(query_rows.reshape(token_count, KVH, ratio, HD), (1, 0, 2, 3))
    key_groups = jnp.transpose(key_all, (1, 0, 2))
    value_groups = jnp.transpose(value_all, (1, 0, 2))

    def one_group(operands):
        query_one, key_one, value_one = operands
        scores = (
            jnp.einsum("qrd,kd->rqk", query_one, key_one, preferred_element_type=jnp.float32)
            * scale
        )
        scores = jnp.where(allowed[None], scores, -jnp.inf)
        highest = jnp.max(scores, axis=-1, keepdims=True)
        probs = jnp.exp(scores - highest)
        probs = (probs / jnp.sum(probs, axis=-1, keepdims=True)).astype(jnp.bfloat16)
        output = jnp.einsum("rqk,kd->qrd", probs, value_one, preferred_element_type=jnp.float32)
        return output.astype(jnp.bfloat16)

    outputs = lax.map(one_group, (query_groups, key_groups, value_groups))
    return jnp.transpose(outputs, (1, 0, 2, 3)).reshape(token_count, QH * HD)


def shards(hidden, queries, norm_gain, kv_weight, value_bias, doc_lengths):
    token_count = hidden.shape[1]
    group_size = lax.axis_size("sp")
    query_rows = queries[0]
    wide = hidden[0].astype(jnp.float32)
    normed = (
        wide * lax.rsqrt(jnp.mean(wide * wide, axis=-1, keepdims=True) + EPS) * norm_gain
    ).astype(jnp.bfloat16)
    projected = jnp.dot(
        normed,
        lax.all_gather(kv_weight, "fsdp", axis=0, tiled=True),
        preferred_element_type=jnp.float32,
    )
    keys = projected[:, : KVH * HD].astype(jnp.bfloat16).reshape(token_count, KVH, HD)
    values = (
        (projected[:, KVH * HD :] + value_bias).astype(jnp.bfloat16).reshape(token_count, KVH, HD)
    )
    ends = jnp.cumsum(doc_lengths[0])
    reach = group_size // 4
    first = lax.axis_index("sp") * token_count
    key_parts = [keys]
    value_parts = [values]
    for back in range(1, reach + 1):
        key_far, value_far = from_behind((keys, values), "sp", back)
        key_parts.insert(0, key_far)
        value_parts.insert(0, value_far)
    key_all = jnp.concatenate(key_parts, axis=0)
    value_all = jnp.concatenate(value_parts, axis=0)
    query_pos = first + jnp.arange(token_count, dtype=jnp.int32)
    key_pos = first - reach * token_count + jnp.arange(key_all.shape[0], dtype=jnp.int32)
    query_ids = jnp.sum((query_pos[:, None] >= ends[None, :]).astype(jnp.int32), axis=1)
    key_ids = jnp.sum((key_pos[:, None] >= ends[None, :]).astype(jnp.int32), axis=1)
    result = attend_near(query_rows, key_all, value_all, query_pos, key_pos, query_ids, key_ids)
    return result.reshape(1, token_count, QH * HD)


def solution(mesh):
    in_specs = (
        P("fsdp", "sp", None),
        P("fsdp", "sp", None),
        P(),
        P("fsdp", None),
        P(),
        P("fsdp", None),
    )
    out_specs = P("fsdp", "sp", None)
    return jax.shard_map(shards, mesh=mesh, in_specs=in_specs, out_specs=out_specs, check_vma=False)
```

profile of v0, /device:TPU:135, one launch (start us, length us, event | category | flops | bytes accessed | tf_op | source)
XLA Modules:
  0.0 336.2 jit_solution(246101491837138390)
XLA Ops:
  8.3 2.3 fusion.50
  10.7 114.0 %all-gather.2.cloned.1.call-done = bf16[5120,2048]{1,0:T(8,128)(2,1)} async-done(((bf16[320,2048]{1,0:T(8,128)(2,1)}), bf16[5120,2048]{1,0:T(8,128)(2,1)}) %all-gather.2.cloned.1.call-update) | async-done | bytes 20971536 | tf_op jit(solution)/shard_map/all_gather | solution.py:60
  124.7 9.9 %fusion.53 = f32[256,2048]{1,0:T(8,128)S(1)} fusion(bf16[5120,2048]{1,0:T(8,128)(2,1)} %all-gather.2.cloned.1.call-done, bf16[1,256,5120]{2,1,0:T(8,128)(2,1)S(1)} %copy-done, f32[5120]{0:T(1024)S(1)} %copy-done.6, f32[256]{0:T(256)S(1)} %add_rsqrt_fusion), kind=kOutput, calls=%fused_computation.37 | convolution fusion | flops 5373952000 | bytes 25711616 | tf_op jit(solution)/shard_map/dot_general | solution.py:58
  134.6 1.3 copy-done.1
  136.3 1.4 collective-permute-start
  137.7 1.3 collective-permute-start.1
  140.4 4.1 %copy.46 = bf16[1,256,4096]{1,2,0:T(8,128)(2,1)} copy(bf16[1,256,4096]{2,1,0:T(8,128)(2,1)} %param.9) | data formatting | bytes 4194304 | tf_op args[1]
  144.5 2.4 collective-permute-start.3
  148.3 5.8 %collective-permute-done = bf16[256,8,128]{0,2,1:T(8,128)(2,1)} collective-permute-done((bf16[256,8,128]{0,2,1:T(8,128)(2,1)S(1)}, bf16[256,8,128]{0,2,1:T(8,128)(2,1)}, u32[]{:S(2)}, u32[]{:S(2)}) %collective-permute-start) | collective-permute-done | bytes 524320 | tf_op jit(solution)/shard_map/ppermute | solution.py:17
  156.4 35.8 %collective-permute-done.1 = bf16[256,8,128]{0,2,1:T(8,128)(2,1)} collective-permute-done((bf16[256,8,128]{0,2,1:T(8,128)(2,1)S(1)}, bf16[256,8,128]{0,2,1:T(8,128)(2,1)}, u32[]{:S(2)}, u32[]{:S(2)}) %collective-permute-start.1) | collective-permute-done | bytes 524320 | tf_op jit(solution)/shard_map/ppermute | solution.py:17
  194.6 32.9 %collective-permute-start.7 = (bf16[256,8,128]{2,0,1:T(8,128)(2,1)S(1)}, bf16[256,8,128]{2,0,1:T(8,128)(2,1)S(1)}, u32[]{:S(2)}, u32[]{:S(2)}) collective-permute-start(bf16[256,8,128]{2,0,1:T(8,128)(2,1)S(1)} %copy_bitcast_fusion), channel_id=1, source_target_pairs={{0,1},{1,2},{2,3},{3,4},{4,5},{5,6},{6,7},{7,8},{8,9},{9,10},{10,1... | collective-permute-start | bytes 1572872 | tf_op jit(solution)/shard_map/ppermute | solution.py:17
  228.9 6.2 %collective-permute-done.6 = bf16[256,8,128]{2,0,1:T(8,128)(2,1)S(1)} collective-permute-done((bf16[256,8,128]{2,0,1:T(8,128)(2,1)S(1)}, bf16[256,8,128]{2,0,1:T(8,128)(2,1)S(1)}, u32[]{:S(2)}, u32[]{:S(2)}) %collective-permute-start.6) | collective-permute-done | bytes 524320 | tf_op jit(solution)/shard_map/ppermute | solution.py:17
  235.2 23.7 %collective-permute-done.7 = bf16[256,8,128]{2,0,1:T(8,128)(2,1)S(1)} collective-permute-done((bf16[256,8,128]{2,0,1:T(8,128)(2,1)S(1)}, bf16[256,8,128]{2,0,1:T(8,128)(2,1)S(1)}, u32[]{:S(2)}, u32[]{:S(2)}) %collective-permute-start.7) | collective-permute-done | bytes 524320 | tf_op jit(solution)/shard_map/ppermute | solution.py:17
  259.1 1.5 copy-done.4
  260.6 64.7 %while.11 = (s32[]{:T(128)}, bf16[8,256,4,128]{1,3,2,0:T(8,128)(2,1)}, bf16[8,1280,128]{1,2,0:T(8,128)(2,1)}, bf16[8,1280,128]{2,1,0:T(8,128)(2,1)}, bf16[8,256,...) while((s32[]{:T(128)}, ...), condition=%wide.region_7.8_spmd.clone, body=%wide.region_4.7_spmd.clone.sunk | while | flops 1019874816 | bytes 2777453 | solution.py:46
  261.6 2.9 exponential_reduce_fusion.2
  264.5 4.2 %fusion.78 = bf16[8,256,4,128]{1,3,2,0:T(8,128)(2,1)} fusion(bf16[8,256,4,128]{1,3,2,0:T(8,128)(2,1)} %get-tuple-element.178, s32[]{:T(128)} %get-tuple-element.177, f32[4,256]{1,0:T(4,128)S(1)} %exponential_reduce_fusion.2, bf16[8,1280,128]{1,2,0:T(8,128)(2,1)} %get-tuple-element.190, pred[256,1280]{0,1:T(8,128)(4,1)S(1)} %compare_and_fusion.2, ...), kind=kOutput, calls=%fused_computation.10.clone.1 | convolution fusion | flops 677775616 | bytes 1513472 | tf_op jit(solution)/shard_map/while/body/eval_jaxpr/rqk,kd->qrd/dot_general | solution.py:43
  269.7 2.9 exponential_reduce_fusion.2
  272.6 4.1 %fusion.78 = bf16[8,256,4,128]{1,3,2,0:T(8,128)(2,1)} fusion(bf16[8,256,4,128]{1,3,2,0:T(8,128)(2,1)} %get-tuple-element.178, s32[]{:T(128)} %get-tuple-element.177, f32[4,256]{1,0:T(4,128)S(1)} %exponential_reduce_fusion.2, bf16[8,1280,128]{1,2,0:T(8,128)(2,1)} %get-tuple-element.190, pred[256,1280]{0,1:T(8,128)(4,1)S(1)} %compare_and_fusion.2, ...), kind=kOutput, calls=%fused_computation.10.clone.1 | convolution fusion | flops 677775616 | bytes 1513472 | tf_op jit(solution)/shard_map/while/body/eval_jaxpr/rqk,kd->qrd/dot_general | solution.py:43
  277.8 2.9 exponential_reduce_fusion.2
  280.6 4.1 %fusion.78 = bf16[8,256,4,128]{1,3,2,0:T(8,128)(2,1)} fusion(bf16[8,256,4,128]{1,3,2,0:T(8,128)(2,1)} %get-tuple-element.178, s32[]{:T(128)} %get-tuple-element.177, f32[4,256]{1,0:T(4,128)S(1)} %exponential_reduce_fusion.2, bf16[8,1280,128]{1,2,0:T(8,128)(2,1)} %get-tuple-element.190, pred[256,1280]{0,1:T(8,128)(4,1)S(1)} %compare_and_fusion.2, ...), kind=kOutput, calls=%fused_computation.10.clone.1 | convolution fusion | flops 677775616 | bytes 1513472 | tf_op jit(solution)/shard_map/while/body/eval_jaxpr/rqk,kd->qrd/dot_general | solution.py:43
  285.8 2.9 exponential_reduce_fusion.2
  288.7 4.2 %fusion.78 = bf16[8,256,4,128]{1,3,2,0:T(8,128)(2,1)} fusion(bf16[8,256,4,128]{1,3,2,0:T(8,128)(2,1)} %get-tuple-element.178, s32[]{:T(128)} %get-tuple-element.177, f32[4,256]{1,0:T(4,128)S(1)} %exponential_reduce_fusion.2, bf16[8,1280,128]{1,2,0:T(8,128)(2,1)} %get-tuple-element.190, pred[256,1280]{0,1:T(8,128)(4,1)S(1)} %compare_and_fusion.2, ...), kind=kOutput, calls=%fused_computation.10.clone.1 | convolution fusion | flops 677775616 | bytes 1513472 | tf_op jit(solution)/shard_map/while/body/eval_jaxpr/rqk,kd->qrd/dot_general | solution.py:43
  293.9 2.9 exponential_reduce_fusion.2
  296.8 4.2 %fusion.78 = bf16[8,256,4,128]{1,3,2,0:T(8,128)(2,1)} fusion(bf16[8,256,4,128]{1,3,2,0:T(8,128)(2,1)} %get-tuple-element.178, s32[]{:T(128)} %get-tuple-element.177, f32[4,256]{1,0:T(4,128)S(1)} %exponential_reduce_fusion.2, bf16[8,1280,128]{1,2,0:T(8,128)(2,1)} %get-tuple-element.190, pred[256,1280]{0,1:T(8,128)(4,1)S(1)} %compare_and_fusion.2, ...), kind=kOutput, calls=%fused_computation.10.clone.1 | convolution fusion | flops 677775616 | bytes 1513472 | tf_op jit(solution)/shard_map/while/body/eval_jaxpr/rqk,kd->qrd/dot_general | solution.py:43
  302.0 2.9 exponential_reduce_fusion.2
  304.9 4.2 %fusion.78 = bf16[8,256,4,128]{1,3,2,0:T(8,128)(2,1)} fusion(bf16[8,256,4,128]{1,3,2,0:T(8,128)(2,1)} %get-tuple-element.178, s32[]{:T(128)} %get-tuple-element.177, f32[4,256]{1,0:T(4,128)S(1)} %exponential_reduce_fusion.2, bf16[8,1280,128]{1,2,0:T(8,128)(2,1)} %get-tuple-element.190, pred[256,1280]{0,1:T(8,128)(4,1)S(1)} %compare_and_fusion.2, ...), kind=kOutput, calls=%fused_computation.10.clone.1 | convolution fusion | flops 677775616 | bytes 1513472 | tf_op jit(solution)/shard_map/while/body/eval_jaxpr/rqk,kd->qrd/dot_general | solution.py:43
  310.1 2.9 exponential_reduce_fusion.2
  313.0 4.2 %fusion.78 = bf16[8,256,4,128]{1,3,2,0:T(8,128)(2,1)} fusion(bf16[8,256,4,128]{1,3,2,0:T(8,128)(2,1)} %get-tuple-element.178, s32[]{:T(128)} %get-tuple-element.177, f32[4,256]{1,0:T(4,128)S(1)} %exponential_reduce_fusion.2, bf16[8,1280,128]{1,2,0:T(8,128)(2,1)} %get-tuple-element.190, pred[256,1280]{0,1:T(8,128)(4,1)S(1)} %compare_and_fusion.2, ...), kind=kOutput, calls=%fused_computation.10.clone.1 | convolution fusion | flops 677775616 | bytes 1513472 | tf_op jit(solution)/shard_map/while/body/eval_jaxpr/rqk,kd->qrd/dot_general | solution.py:43
  318.2 2.9 exponential_reduce_fusion.2
  321.1 4.2 %fusion.78 = bf16[8,256,4,128]{1,3,2,0:T(8,128)(2,1)} fusion(bf16[8,256,4,128]{1,3,2,0:T(8,128)(2,1)} %get-tuple-element.178, s32[]{:T(128)} %get-tuple-element.177, f32[4,256]{1,0:T(4,128)S(1)} %exponential_reduce_fusion.2, bf16[8,1280,128]{1,2,0:T(8,128)(2,1)} %get-tuple-element.190, pred[256,1280]{0,1:T(8,128)(4,1)S(1)} %compare_and_fusion.2, ...), kind=kOutput, calls=%fused_computation.10.clone.1 | convolution fusion | flops 677775616 | bytes 1513472 | tf_op jit(solution)/shard_map/while/body/eval_jaxpr/rqk,kd->qrd/dot_general | solution.py:43
  325.3 4.1 %copy.51 = bf16[1,256,4096]{2,1,0:T(8,128)(2,1)} copy(bf16[1,256,4096]{1,2,0:T(8,128)(2,1)} %bitcast.93) | data formatting | bytes 4194304 | tf_op jit(solution)/shard_map/reshape;reshape | solution.py:83
  (53 shorter events, 19.3 us)
Async XLA Ops:
  6.5 118.2 %copy-start = (bf16[1,256,5120]{2,1,0:T(8,128)(2,1)S(1)}, bf16[1,256,5120]{2,1,0:T(8,128)(2,1)}, u32[]{:S(2)}) copy-start(bf16[1,256,5120]{2,1,0:T(8,128)(2,1)} %param.8) | copy-start | bytes 7864324
  6.5 118.2 %copy-start.6 = (f32[5120]{0:T(1024)S(1)}, f32[5120]{0:T(1024)}, u32[]{:S(2)}) copy-start(f32[5120]{0:T(1024)} %param.10) | copy-start | bytes 61444
  6.5 118.2 %all-gather.2.cloned.1.call-start = ((), (), s32[]{:S(2)}) async-start(), calls=%async_computation | async-start | bytes 22282240 | tf_op jit(solution)/shard_map/all_gather | solution.py:60
  10.7 125.3 %copy-start.5 = (f32[1024]{0:T(1024)S(1)}, f32[1024]{0:T(1024)}, u32[]{:S(2)}) copy-start(f32[1024]{0:T(1024)} %param.12) | copy-start | bytes 12292
  134.6 1.3 copy-start.1
  136.0 10.8 %copy-start.2 = (f32[256,2048]{1,0:T(8,128)S(1)}, f32[256,2048]{1,0:T(8,128)}, u32[]{:S(2)}) copy-start(f32[256,2048]{1,0:T(8,128)} %copy-done.1) | copy-start | bytes 6291460
  136.3 17.8 %collective-permute-start = (bf16[256,8,128]{0,2,1:T(8,128)(2,1)S(1)}, bf16[256,8,128]{0,2,1:T(8,128)(2,1)}, u32[]{:S(2)}, u32[]{:S(2)}) collective-permute-start(bf16[256,8,128]{0,2,1:T(8,128)(2,1)S(1)} %bitcast.94), channel_id=1, source_target_pairs={{0,4},{1,5},{2,6},{3,7},{4,8},{5,9},{6,10},{7,11},{8,12},{9,13},{1... | collective-permute-start | bytes 1572872 | tf_op jit(solution)/shard_map/ppermute | solution.py:17
  137.7 54.5 %collective-permute-start.1 = (bf16[256,8,128]{0,2,1:T(8,128)(2,1)S(1)}, bf16[256,8,128]{0,2,1:T(8,128)(2,1)}, u32[]{:S(2)}, u32[]{:S(2)}) collective-permute-start(bf16[256,8,128]{0,2,1:T(8,128)(2,1)S(1)} %bitcast.95), channel_id=1, source_target_pairs={{0,3},{1,4},{2,5},{3,6},{4,7},{5,8},{6,9},{7,10},{8,11},{9,12},{10... | collective-permute-start | bytes 1572872 | tf_op jit(solution)/shard_map/ppermute | solution.py:17
  139.1 55.5 %collective-permute-start.2 = (bf16[256,8,128]{0,2,1:T(8,128)(2,1)S(1)}, bf16[256,8,128]{0,2,1:T(8,128)(2,1)}, u32[]{:S(2)}, u32[]{:S(2)}) collective-permute-start(bf16[256,8,128]{0,2,1:T(8,128)(2,1)S(1)} %bitcast.96), channel_id=1, source_target_pairs={{0,2},{1,3},{2,4},{3,5},{4,6},{5,7},{6,8},{7,9},{8,10},{9,11},{10,... | collective-permute-start | bytes 1572872 | tf_op jit(solution)/shard_map/ppermute | solution.py:17
  144.5 84.1 %collective-permute-start.3 = (bf16[256,8,128]{0,2,1:T(8,128)(2,1)S(1)}, bf16[256,8,128]{0,2,1:T(8,128)(2,1)S(1)}, u32[]{:S(2)}, u32[]{:S(2)}) collective-permute-start(bf16[256,8,128]{0,2,1:T(8,128)(2,1)S(1)} %bitcast.97), channel_id=1, source_target_pairs={{0,1},{1,2},{2,3},{3,4},{4,5},{5,6},{6,7},{7,8},{8,9},{9,10},{10,1... | collective-permute-start | bytes 1572872 | tf_op jit(solution)/shard_map/ppermute | solution.py:17
  147.0 81.8 %collective-permute-start.4 = (bf16[256,8,128]{2,0,1:T(8,128)(2,1)S(1)}, bf16[256,8,128]{2,0,1:T(8,128)(2,1)S(1)}, u32[]{:S(2)}, u32[]{:S(2)}) collective-permute-start(bf16[256,8,128]{2,0,1:T(8,128)(2,1)S(1)} %copy_bitcast_fusion), channel_id=1, source_target_pairs={{0,4},{1,5},{2,6},{3,7},{4,8},{5,9},{6,10},{7,11},{8,12},{9,13},{1... | collective-permute-start | bytes 1572872 | tf_op jit(solution)/shard_map/ppermute | solution.py:17
  154.0 74.7 %collective-permute-start.5 = (bf16[256,8,128]{2,0,1:T(8,128)(2,1)S(1)}, bf16[256,8,128]{2,0,1:T(8,128)(2,1)S(1)}, u32[]{:S(2)}, u32[]{:S(2)}) collective-permute-start(bf16[256,8,128]{2,0,1:T(8,128)(2,1)S(1)} %copy_bitcast_fusion), channel_id=1, source_target_pairs={{0,3},{1,4},{2,5},{3,6},{4,7},{5,8},{6,9},{7,10},{8,11},{9,12},{10... | collective-permute-start | bytes 1572872 | tf_op jit(solution)/shard_map/ppermute | solution.py:17
  192.3 42.8 %collective-permute-start.6 = (bf16[256,8,128]{2,0,1:T(8,128)(2,1)S(1)}, bf16[256,8,128]{2,0,1:T(8,128)(2,1)S(1)}, u32[]{:S(2)}, u32[]{:S(2)}) collective-permute-start(bf16[256,8,128]{2,0,1:T(8,128)(2,1)S(1)} %copy_bitcast_fusion), channel_id=1, source_target_pairs={{0,2},{1,3},{2,4},{3,5},{4,6},{5,7},{6,8},{7,9},{8,10},{9,11},{10,... | collective-permute-start | bytes 1572872 | tf_op jit(solution)/shard_map/ppermute | solution.py:17
  194.6 64.2 %collective-permute-start.7 = (bf16[256,8,128]{2,0,1:T(8,128)(2,1)S(1)}, bf16[256,8,128]{2,0,1:T(8,128)(2,1)S(1)}, u32[]{:S(2)}, u32[]{:S(2)}) collective-permute-start(bf16[256,8,128]{2,0,1:T(8,128)(2,1)S(1)} %copy_bitcast_fusion), channel_id=1, source_target_pairs={{0,1},{1,2},{2,3},{3,4},{4,5},{5,6},{6,7},{7,8},{8,9},{9,10},{10,1... | collective-permute-start | bytes 1572872 | tf_op jit(solution)/shard_map/ppermute | solution.py:17
  228.7 30.3 %copy-start.3 = (bf16[1280,8,128]{0,2,1:T(8,128)(2,1)}, bf16[1280,8,128]{0,2,1:T(8,128)(2,1)S(1)}, u32[]{:S(2)}) copy-start(bf16[1280,8,128]{0,2,1:T(8,128)(2,1)S(1)} %constant_dynamic-update-slice_fusion) | copy-start | bytes 7864324
  259.1 1.5 copy-start.4
Sparse Core Ops, SparseCore 0:
  9.2 115.4 all-gather.1
where the time goes:
time: 337 us; the launch traced here: 336 us
  waiting for transfers between devices  186 us (55%)
  matrix products  66.3 us (20%)
  starting transfers between devices  43.1 us (13%)
  local copies, waits for them, and re-layouts  15.8 us (5%)
  between operations  13.7 us (4%)
  other arithmetic  11 us (3%)
    all_gather x1, waiting for transfers between devices, shards(): lax.all_gather(kv_weight, 'fsdp', axis=0, tiled=True)  114 us
    ppermute x8, waiting for transfers between devices, from_behind(): return lax.ppermute(value, axis, pairs)  71.5 us
    ppermute x8, starting transfers between devices, from_behind(): return lax.ppermute(value, axis, pairs)  43.1 us
    dot_general x8, matrix products, one_group(): jnp.einsum('rqk,kd->qrd', probs, value_one, preferred_element_type=jnp.fl...  33.3 us
    sub x8, matrix products, one_group(): probs = jnp.exp(scores - highest)  23.1 us
    unnamed x23, local copies, waits for them, and re-layouts  10.5 us
    dot_general x1, matrix products, shards(): jnp.dot(normed, lax.all_gather(kv_weight, 'fsdp', axis=0, tiled=True), pr...  9.9 us
    and x8, other arithmetic, attend_near(): (key_pos[None, :] >= 0) & (key_pos[None, :] <= query_pos[:, None])  8.24 us
  transfers between devices with their start and end apart: 9, of which 5 were waited for; matrix products, arithmetic and copies ran while one was open for 3% of the time, Pallas kernels for 0%

commit v1 on v0

v1 whole, which is shorter than its diff:
```python
import jax
import jax.numpy as jnp
from jax import lax
from jax.experimental import pallas as pl
from jax.experimental.pallas import tpu as pltpu
from jax.sharding import PartitionSpec as P

QH = 32
KVH = 8
HD = 128
D = 5120
T = 256
NDOC = 16
RATIO = QH // KVH
ROWS = D // 16
QUART = ROWS // 4
WIN = 5 * T
EPS = 1e-06
LOG2E = 1.4426950408889634
MESH = pl.DeviceIdType.MESH

YA, ZA, YB, XC, EC, XP, ZU, ZD, RU, RD = 0, 3, 4, 7, 10, 11, 12, 13, 14, 15
KINDS = 16


def kernel(
    dl_ref, hid_hbm, q_hbm, gain_ref, w_hbm, vb_ref, out_hbm,
    wbuf, nbuf, qbuf, kvbuf, bias, obuf,
    w_sem, in_sem, out_sem, send, recv,
):
    f = lax.axis_index("fsdp")
    s = lax.axis_index("sp")
    y, zl, c = f // 4, lax.rem(f // 2, 2), lax.rem(f, 2)
    x, zh = s // 4, lax.rem(s, 4)

    def dev(yy, zz, cc, xx, hh):
        return {"fsdp": (yy * 2 + zz) * 2 + cc, "sp": xx * 4 + hh}

    def y_at(d):
        return dev(lax.rem(y + d, 4), zl, c, x, zh)

    def x_at(d):
        return dev(y, zl, c, lax.rem(x + d, 4), zh)

    def h_at(d):
        return dev(y, zl, c, x, lax.rem(zh + d, 4))

    z_pair = dev(y, 1 - zl, c, x, zh)
    core_pair = dev(y, zl, 1 - c, x, zh)
    quarter = pl.ds(pl.multiple_of(x * QUART, 16), QUART)

    def remote(src, dst, kind, h, device, recv_kind=None):
        return pltpu.make_async_remote_copy(
            src_ref=src,
            dst_ref=dst,
            send_sem=send.at[kind, h],
            recv_sem=recv.at[kind if recv_kind is None else recv_kind, h],
            device_id=device,
            device_id_type=MESH,
        )

    def ya(h, d):
        own = wbuf.at[h, y, zl, c]
        return remote(own, own, YA + d - 1, h, y_at(d))

    def za(h):
        part = wbuf.at[h, y, zl, c, quarter]
        return remote(part, part, ZA, h, z_pair)

    def yb(h, d):
        part = wbuf.at[h, y, 1 - zl, c, quarter]
        return remote(part, part, YB + d - 1, h, y_at(d))

    def xc(h, d):
        part = wbuf.at[h, :, 1 - zl, c, quarter]
        return remote(part, part, XC + d - 1, h, x_at(d))

    def ec(h):
        half = wbuf.at[h, :, :, c]
        return remote(half, half, EC, h, core_pair)

    def xp(h):
        return remote(kvbuf.at[h, 4], kvbuf.at[h, 0], XP, h, x_at(1))

    def zu(h):
        return remote(kvbuf.at[h, jnp.where(zh < 3, 4, 0)], kvbuf.at[h, 3], ZU, h, h_at(1))

    def zd(h):
        return remote(kvbuf.at[h, jnp.where(zh > 0, 0, 4)], kvbuf.at[h, 1], ZD, h, h_at(3))

    def ru(h):
        return remote(kvbuf.at[h, 3], kvbuf.at[h, 2], RU, h, h_at(1), RU)

    def rd(h):
        return remote(kvbuf.at[h, 1], kvbuf.at[h, 2], RD, h, h_at(3), RU)

    def w_local(h, part):
        columns = pl.ds(pl.multiple_of(part * KVH * HD + h * HD, HD), HD)
        return pltpu.make_async_copy(
            w_hbm.at[:, columns],
            wbuf.at[h, y, zl, c, :, pl.ds(part * HD, HD)],
            w_sem.at[part, h],
        )

    def out_copy(h):
        columns = pl.ds(pl.multiple_of(h * RATIO * HD, HD), RATIO * HD)
        return pltpu.make_async_copy(obuf.at[:, columns], out_hbm.at[:, columns], out_sem.at[h])

    hid_copy = pltpu.make_async_copy(hid_hbm, nbuf, in_sem.at[0])
    q_copy = pltpu.make_async_copy(q_hbm, qbuf, in_sem.at[1])

    @pl.loop(0, KVH)
    def _(h):
        w_local(h, 0).start()
        w_local(h, 1).start()

    hid_copy.start()
    q_copy.start()

    barrier = pltpu.get_barrier_semaphore()
    partners = [y_at(1), y_at(2), y_at(3), x_at(1), x_at(2), x_at(3), h_at(1), h_at(3), z_pair, core_pair]
    for device in partners:
        pl.semaphore_signal(barrier, inc=1, device_id=device, device_id_type=MESH)
    pl.semaphore_wait(barrier, len(partners))

    def start_a(h):
        w_local(h, 0).wait()
        w_local(h, 1).wait()
        za(h).start()
        for d in (1, 3, 2):
            ya(h, d).start()

    def start_b(h):
        za(h).wait_recv()
        for d in (1, 3, 2):
            yb(h, d).start()

    def start_c(h):
        for d in (1, 2, 3):
            yb(h, d).wait_recv()
        for d in (1, 3, 2):
            xc(h, d).start()

    def start_e(h):
        for d in (1, 2, 3):
            ya(h, d).wait_recv()
        for d in (1, 2, 3):
            xc(h, d).wait_recv()
        ec(h).start()

    def project(h):
        ec(h).wait_recv()
        weight = wbuf[h].reshape(D, 2 * HD)
        result = jnp.dot(nbuf[...], weight, preferred_element_type=jnp.float32)
        kvbuf[h, 4, :, pl.ds(0, HD)] = result[:, :HD].astype(jnp.bfloat16)
        kvbuf[h, 4, :, pl.ds(HD, HD)] = (result[:, HD:] + vb_ref[pl.ds(h, 1), :]).astype(jnp.bfloat16)

    def attend(h, first_head, count):
        key = kvbuf[h, :, :, pl.ds(0, HD)].reshape(WIN, HD)
        value = kvbuf[h, :, :, pl.ds(HD, HD)].reshape(WIN, HD)
        for r in range(first_head, first_head + count):
            columns = pl.ds(pl.multiple_of((h * RATIO + r) * HD, HD), HD)
            scores = lax.dot_general(
                qbuf[:, columns], key, (((1,), (1,)), ((), ())), preferred_element_type=jnp.float32
            )
            scores = scores * (HD**-0.5 * LOG2E) + bias[...]
            highest = jnp.max(scores, axis=-1, keepdims=True)
            probs = jnp.exp2(scores - highest)
            total = jnp.sum(probs, axis=-1, keepdims=True)
            output = jnp.dot(probs.astype(jnp.bfloat16), value, preferred_element_type=jnp.float32)
            obuf[:, columns] = (output / total).astype(jnp.bfloat16)

    start_a(0)

    hid_copy.wait()

    @pl.loop(0, T // 16)
    def _(i):
        rows = pl.ds(pl.multiple_of(i * 16, 16), 16)
        wide = nbuf[rows, :].astype(jnp.float32)
        square = jnp.mean(wide * wide, axis=-1, keepdims=True)
        nbuf[rows, :] = (wide * lax.rsqrt(square + EPS) * gain_ref[...]).astype(jnp.bfloat16)

    start_b(0)
    start_a(1)

    first = s * T
    query_pos = first + lax.broadcasted_iota(jnp.int32, (T, 1), 0)
    begin = jnp.zeros((T, 1), jnp.int32)
    end = dl_ref[0, 0]
    for d in range(NDOC):
        begin = jnp.where(query_pos >= end, end, begin)
        if d + 1 < NDOC:
            end = end + dl_ref[0, d + 1]
    key_pos = first - 4 * T + lax.broadcasted_iota(jnp.int32, (T, WIN), 1)
    bias[...] = jnp.where((key_pos <= query_pos) & (key_pos >= begin), 0.0, -jnp.inf)

    start_c(0)
    q_copy.wait()

    @pl.loop(0, KVH + 2)
    def _(i):
        @pl.when(i < KVH)
        def _():
            start_e(i)

        @pl.when(i + 1 < KVH)
        def _():
            start_b(i + 1)

        @pl.when(i >= 2)
        def _():
            ru(i - 2).wait_recv()
            attend(i - 2, 0, 2)

        @pl.when(i < KVH)
        def _():
            project(i)
            xp(i).start()

            @pl.when(zh < 3)
            def _():
                zu(i).start()

            @pl.when(zh == 0)
            def _():
                zd(i).start()

        @pl.when(i + 1 < KVH)
        def _():
            start_c(i + 1)

        @pl.when(i + 2 < KVH)
        def _():
            start_a(i + 2)

        @pl.when(i >= 2)
        def _():
            attend(i - 2, 2, 2)
            out_copy(i - 2).start()

        @pl.when(i < KVH)
        def _():
            xp(i).wait_recv()

            @pl.when(zh == 3)
            def _():
                zu(i).start()

            @pl.when(zh > 0)
            def _():
                zd(i).start()

        @pl.when((i >= 1) & (i <= KVH))
        def _():
            zu(i - 1).wait_recv()
            zd(i - 1).wait_recv()

            @pl.when((zh == 1) | (zh == 2))
            def _():
                ru(i - 1).start()
                rd(i - 1).start()

    @pl.loop(0, KVH)
    def _(h):
        for d in (1, 2, 3):
            ya(h, d).wait_send()
            yb(h, d).wait_send()
            xc(h, d).wait_send()
        za(h).wait_send()
        ec(h).wait_send()
        xp(h).wait_send()
        zu(h).wait_send()
        zd(h).wait_send()

        @pl.when((zh == 1) | (zh == 2))
        def _():
            ru(h).wait_send()
            rd(h).wait_send()

        out_copy(h).wait()


def shards(hidden, queries, norm_gain, kv_weight, value_bias, doc_lengths):
    anywhere = pl.BlockSpec(memory_space=pl.ANY)
    vmem = pl.BlockSpec(memory_space=pltpu.VMEM)
    out = pl.pallas_call(
        kernel,
        out_shape=jax.ShapeDtypeStruct((T, QH * HD), jnp.bfloat16),
        in_specs=[pl.BlockSpec(memory_space=pltpu.SMEM), anywhere, anywhere, vmem, anywhere, vmem],
        out_specs=anywhere,
        scratch_shapes=[
            pltpu.VMEM((KVH, 4, 2, 2, ROWS, 2 * HD), jnp.bfloat16),
            pltpu.VMEM((T, D), jnp.bfloat16),
            pltpu.VMEM((T, QH * HD), jnp.bfloat16),
            pltpu.VMEM((KVH, 5, T, 2 * HD), jnp.bfloat16),
            pltpu.VMEM((T, WIN), jnp.float32),
            pltpu.VMEM((T, QH * HD), jnp.bfloat16),
            pltpu.SemaphoreType.DMA((2, KVH)),
            pltpu.SemaphoreType.DMA((2,)),
            pltpu.SemaphoreType.DMA((KVH,)),
            pltpu.SemaphoreType.DMA((KINDS, KVH)),
            pltpu.SemaphoreType.DMA((KINDS, KVH)),
        ],
        compiler_params=pltpu.CompilerParams(
            collective_id=0, has_side_effects=True, vmem_limit_bytes=60 * 1024 * 1024
        ),
    )(
        doc_lengths,
        hidden[0],
        queries[0],
        norm_gain.reshape(1, D),
        kv_weight,
        value_bias.reshape(KVH, HD),
    )
    return out.reshape(1, T, QH * HD)


def solution(mesh):
    in_specs = (
        P("fsdp", "sp", None),
        P("fsdp", "sp", None),
        P(),
        P("fsdp", None),
        P(),
        P("fsdp", None),
    )
    out_specs = P("fsdp", "sp", None)
    return jax.shard_map(shards, mesh=mesh, in_specs=in_specs, out_specs=out_specs, check_vma=False)
```

time: 337 us -> 185 us (0.55)
  the two profiles are of different devices: /device:TPU:135 before, /device:TPU:7 now
where the time goes in v1:
time: 185 us
  Pallas kernels  182 us (98%)
  local copies, waits for them, and re-layouts  3.13 us (2%)
    pallas_call x1, Pallas kernels, shards(): pl.pallas_call(kernel, out_shape=jax.ShapeDtypeStruct((T, QH * HD), jnp.b...  182 us

profile of v1, /device:TPU:7, one launch (start us, length us, event | category | flops | bytes accessed | tf_op | source)
XLA Modules:
  0.0 185.0 jit_solution(3399683614363858321)
XLA Ops:
  0.0 181.9 %shard_map.64 = bf16[256,4096]{1,0:T(8,128)(2,1)} custom-call(s32[1,16]{1,0:T(1,128)} %dl_ref.1, bf16[256,5120]{1,0:T(8,128)(2,1)} %bitcast.6, bf16[256,4096]{1,0:T(8,128)(2,1)} %bitcast.7, f32[1,5120]{1,0:T(1,128)} %bitcast.8, bf16[320,2048]{1,0:T(8,128)(2,1)} %w_hbm.1, f32[8,128]{1,0:T(8,128)} %bitcast.9), custom_call_target="tpu_custom_call" | custom-call | tf_op jit(solution)/shard_map/pallas_call | solution.py:287
  181.9 3.1 %copy.8 = bf16[1,256,4096]{2,1,0:T(8,128)(2,1)} copy(bf16[1,256,4096]{2,1,0:T(8,128)(2,1)} %bitcast.5) | data formatting | bytes 4194304

commit v2 on v1

--- a/solution.py
+++ b/solution.py
@@ -19,8 +19,8 @@
 LOG2E = 1.4426950408889634
 MESH = pl.DeviceIdType.MESH
 
-YA, ZA, YB, XC, EC, XP, ZU, ZD, RU, RD = 0, 3, 4, 7, 10, 11, 12, 13, 14, 15
-KINDS = 16
+YA, ZA, YB, XC, EC, XP, ZU, ZD, ZT = 0, 3, 4, 7, 10, 11, 12, 13, 14
+KINDS = 15
 
 
 def kernel(
@@ -46,15 +46,17 @@
         return dev(y, zl, c, x, lax.rem(zh + d, 4))
 
     z_pair = dev(y, 1 - zl, c, x, zh)
+    z_beside = lax.rem(zh + 3 + 2 * zl, 4)
+    z_other = dev(y, 1 - zl, c, x, z_beside)
     core_pair = dev(y, zl, 1 - c, x, zh)
     quarter = pl.ds(pl.multiple_of(x * QUART, 16), QUART)
 
-    def remote(src, dst, kind, h, device, recv_kind=None):
+    def remote(src, dst, kind, h, device):
         return pltpu.make_async_remote_copy(
             src_ref=src,
             dst_ref=dst,
             send_sem=send.at[kind, h],
-            recv_sem=recv.at[kind if recv_kind is None else recv_kind, h],
+            recv_sem=recv.at[kind, h],
             device_id=device,
             device_id_type=MESH,
         )
@@ -65,7 +67,7 @@
 
     def za(h):
         part = wbuf.at[h, y, zl, c, quarter]
-        return remote(part, part, ZA, h, z_pair)
+        return remote(part, part, ZA, h, dev(y, 1 - zl, c, x, jnp.where(lax.rem(h, 2) == 0, zh, z_beside)))
 
     def yb(h, d):
         part = wbuf.at[h, y, 1 - zl, c, quarter]
@@ -88,11 +90,8 @@
     def zd(h):
         return remote(kvbuf.at[h, jnp.where(zh > 0, 0, 4)], kvbuf.at[h, 1], ZD, h, h_at(3))
 
-    def ru(h):
-        return remote(kvbuf.at[h, 3], kvbuf.at[h, 2], RU, h, h_at(1), RU)
-
-    def rd(h):
-        return remote(kvbuf.at[h, 1], kvbuf.at[h, 2], RD, h, h_at(3), RU)
+    def zt(h):
+        return remote(kvbuf.at[h, jnp.where(zh < 2, 4, 0)], kvbuf.at[h, 2], ZT, h, h_at(2))
 
     def w_local(h, part):
         columns = pl.ds(pl.multiple_of(part * KVH * HD + h * HD, HD), HD)
@@ -118,16 +117,16 @@
     q_copy.start()
 
     barrier = pltpu.get_barrier_semaphore()
-    partners = [y_at(1), y_at(2), y_at(3), x_at(1), x_at(2), x_at(3), h_at(1), h_at(3), z_pair, core_pair]
+    partners = [y_at(1), y_at(2), y_at(3), x_at(1), x_at(2), x_at(3), h_at(1), h_at(2), h_at(3), z_pair, z_other, core_pair]
     for device in partners:
         pl.semaphore_signal(barrier, inc=1, device_id=device, device_id_type=MESH)
     pl.semaphore_wait(barrier, len(partners))
 
-    def start_a(h):
+    def start_a(h, offsets=(1, 3, 2)):
         w_local(h, 0).wait()
         w_local(h, 1).wait()
         za(h).start()
-        for d in (1, 3, 2):
+        for d in offsets:
             ya(h, d).start()
 
     def start_b(h):
@@ -155,10 +154,43 @@
         kvbuf[h, 4, :, pl.ds(0, HD)] = result[:, :HD].astype(jnp.bfloat16)
         kvbuf[h, 4, :, pl.ds(HD, HD)] = (result[:, HD:] + vb_ref[pl.ds(h, 1), :]).astype(jnp.bfloat16)
 
-    def attend(h, first_head, count):
+    def send_own(h):
+        xp(h).start()
+
+        @pl.when(zh < 3)
+        def _():
+            zu(h).start()
+
+        @pl.when(zh < 2)
+        def _():
+            zt(h).start()
+
+        @pl.when(zh == 0)
+        def _():
+            zd(h).start()
+
+    def send_previous(h):
+        xp(h).wait_recv()
+
+        @pl.when(zh > 0)
+        def _():
+            zd(h).start()
+
+        @pl.when(zh >= 2)
+        def _():
+            zt(h).start()
+
+        @pl.when(zh == 3)
+        def _():
+            zu(h).start()
+
+    def attend(h):
+        zu(h).wait_recv()
+        zd(h).wait_recv()
+        zt(h).wait_recv()
         key = kvbuf[h, :, :, pl.ds(0, HD)].reshape(WIN, HD)
         value = kvbuf[h, :, :, pl.ds(HD, HD)].reshape(WIN, HD)
-        for r in range(first_head, first_head + count):
+        for r in range(RATIO):
             columns = pl.ds(pl.multiple_of((h * RATIO + r) * HD, HD), HD)
             scores = lax.dot_general(
                 qbuf[:, columns], key, (((1,), (1,)), ((), ())), preferred_element_type=jnp.float32
@@ -169,20 +201,9 @@
             total = jnp.sum(probs, axis=-1, keepdims=True)
             output = jnp.dot(probs.astype(jnp.bfloat16), value, preferred_element_type=jnp.float32)
             obuf[:, columns] = (output / total).astype(jnp.bfloat16)
-
-    start_a(0)
-
-    hid_copy.wait()
-
-    @pl.loop(0, T // 16)
-    def _(i):
-        rows = pl.ds(pl.multiple_of(i * 16, 16), 16)
-        wide = nbuf[rows, :].astype(jnp.float32)
-        square = jnp.mean(wide * wide, axis=-1, keepdims=True)
-        nbuf[rows, :] = (wide * lax.rsqrt(square + EPS) * gain_ref[...]).astype(jnp.bfloat16)
-
-    start_b(0)
-    start_a(1)
+        out_copy(h).start()
+
+    start_a(0, (1, 3))
 
     first = s * T
     query_pos = first + lax.broadcasted_iota(jnp.int32, (T, 1), 0)
@@ -195,71 +216,38 @@
     key_pos = first - 4 * T + lax.broadcasted_iota(jnp.int32, (T, WIN), 1)
     bias[...] = jnp.where((key_pos <= query_pos) & (key_pos >= begin), 0.0, -jnp.inf)
 
-    start_c(0)
+    start_b(0)
+    ya(0, 2).start()
+    start_a(1)
+    hid_copy.wait()
+
+    @pl.loop(0, T // 16)
+    def _(i):
+        rows = pl.ds(pl.multiple_of(i * 16, 16), 16)
+        wide = nbuf[rows, :].astype(jnp.float32)
+        square = jnp.mean(wide * wide, axis=-1, keepdims=True)
+        nbuf[rows, :] = (wide * lax.rsqrt(square + EPS) * gain_ref[...]).astype(jnp.bfloat16)
+
     q_copy.wait()
 
-    @pl.loop(0, KVH + 2)
+    stages = [
+        (5, send_previous),
+        (4, project),
+        (4, send_own),
+        (3, start_e),
+        (2, start_c),
+        (1, start_b),
+        (0, start_a),
+        (8, attend),
+    ]
+
+    @pl.loop(2, KVH + 8)
     def _(i):
-        @pl.when(i < KVH)
-        def _():
-            start_e(i)
-
-        @pl.when(i + 1 < KVH)
-        def _():
-            start_b(i + 1)
-
-        @pl.when(i >= 2)
-        def _():
-            ru(i - 2).wait_recv()
-            attend(i - 2, 0, 2)
-
-        @pl.when(i < KVH)
-        def _():
-            project(i)
-            xp(i).start()
-
-            @pl.when(zh < 3)
-            def _():
-                zu(i).start()
-
-            @pl.when(zh == 0)
-            def _():
-                zd(i).start()
-
-        @pl.when(i + 1 < KVH)
-        def _():
-            start_c(i + 1)
-
-        @pl.when(i + 2 < KVH)
-        def _():
-            start_a(i + 2)
-
-        @pl.when(i >= 2)
-        def _():
-            attend(i - 2, 2, 2)
-            out_copy(i - 2).start()
-
-        @pl.when(i < KVH)
-        def _():
-            xp(i).wait_recv()
-
-            @pl.when(zh == 3)
-            def _():
-                zu(i).start()
-
-            @pl.when(zh > 0)
-            def _():
-                zd(i).start()
-
-        @pl.when((i >= 1) & (i <= KVH))
-        def _():
-            zu(i - 1).wait_recv()
-            zd(i - 1).wait_recv()
-
-            @pl.when((zh == 1) | (zh == 2))
-            def _():
-                ru(i - 1).start()
-                rd(i - 1).start()
+        for lag, stage in stages:
+
+            @pl.when((i >= lag) & (i < KVH + lag))
+            def _(lag=lag, stage=stage):
+                stage(i - lag)
 
     @pl.loop(0, KVH)
     def _(h):
@@ -273,11 +261,7 @@
         zu(h).wait_send()
         zd(h).wait_send()
 
-        @pl.when((zh == 1) | (zh == 2))
-        def _():
-            ru(h).wait_send()
-            rd(h).wait_send()
-
+        zt(h).wait_send()
         out_copy(h).wait()
 
 

time: 185 us -> 151 us (0.82)
  the two profiles are of different devices: /device:TPU:7 before, /device:TPU:32 now
where the time goes in v2:
time: 151 us
  Pallas kernels  147 us (97%)
  local copies, waits for them, and re-layouts  3.13 us (2%)
    pallas_call x1, Pallas kernels, shards(): pl.pallas_call(kernel, out_shape=jax.ShapeDtypeStruct((T, QH * HD), jnp.b...  147 us
    unnamed x1, local copies, waits for them, and re-layouts  3.13 us

profile of v2, /device:TPU:32, one launch (start us, length us, event | category | flops | bytes accessed | tf_op | source)
XLA Modules:
  0.0 150.5 jit_solution(11938991341232952399)
XLA Ops:
  0.0 147.4 %shard_map.64 = bf16[256,4096]{1,0:T(8,128)(2,1)} custom-call(s32[1,16]{1,0:T(1,128)} %dl_ref.1, bf16[256,5120]{1,0:T(8,128)(2,1)} %bitcast.6, bf16[256,4096]{1,0:T(8,128)(2,1)} %bitcast.7, f32[1,5120]{1,0:T(1,128)} %bitcast.8, bf16[320,2048]{1,0:T(8,128)(2,1)} %w_hbm.1, f32[8,128]{1,0:T(8,128)} %bitcast.9), custom_call_target="tpu_custom_call" | custom-call | tf_op jit(solution)/shard_map/pallas_call | solution.py:271
  147.4 3.1 %copy.8 = bf16[1,256,4096]{2,1,0:T(8,128)(2,1)} copy(bf16[1,256,4096]{2,1,0:T(8,128)(2,1)} %bitcast.5) | data formatting | bytes 4194304

commit v3 on v2

--- a/solution.py
+++ b/solution.py
@@ -19,8 +19,21 @@
 LOG2E = 1.4426950408889634
 MESH = pl.DeviceIdType.MESH
 
-YA, ZA, YB, XC, EC, XP, ZU, ZD, ZT = 0, 3, 4, 7, 10, 11, 12, 13, 14
-KINDS = 15
+YA, ZA, YB, XC, EC, XP, ZU, ZD, ZT = 0, 3, 4, 7, 10, 12, 13, 14, 15
+KINDS = 16
+
+
+RUNS = (
+    ("A0", "B0", "A1", "B1", "M0", "A2.0", "C0", "C2.0", "N0", "A2", "A2.1", "C1", "B2", "C2.1", "A3", "E1.0", "E2.0",),
+    ("C2", "A2.2", "B3", "E1.1", "E2.1", "A2.3", "C2.2", "V0",),
+    ("A4", "E1.2", "B4", "A5", "C3", "E2.2", "A6", "V1", "E1.3", "A7", "C2.3", "B5",),
+    ("A2.4", "C4", "A2.5", "E2.3", "V2", "C2.4", "B6",),
+    ("C5", "E1.4", "E2.4", "B7", "C2.5", "V3",),
+    ("A2.6", "C6", "E1.5", "A2.7", "E2.5", "C2.6", "E1.6", "V4",),
+    ("C7", "C2.7", "E2.6", "V5", "E1.7",),
+    ("V6", "E2.7",),
+    ("V7",),
+)
 
 
 def kernel(
@@ -77,9 +90,9 @@
         part = wbuf.at[h, :, 1 - zl, c, quarter]
         return remote(part, part, XC + d - 1, h, x_at(d))
 
-    def ec(h):
-        half = wbuf.at[h, :, :, c]
-        return remote(half, half, EC, h, core_pair)
+    def ec(h, other):
+        part = wbuf.at[h, :, 1 - zl if other else zl, c]
+        return remote(part, part, EC + other, h, core_pair)
 
     def xp(h):
         return remote(kvbuf.at[h, 4], kvbuf.at[h, 0], XP, h, x_at(1))
@@ -122,12 +135,15 @@
         pl.semaphore_signal(barrier, inc=1, device_id=device, device_id_type=MESH)
     pl.semaphore_wait(barrier, len(partners))
 
-    def start_a(h, offsets=(1, 3, 2)):
+    def start_a(h):
         w_local(h, 0).wait()
         w_local(h, 1).wait()
         za(h).start()
-        for d in offsets:
-            ya(h, d).start()
+        ya(h, 1).start()
+        ya(h, 3).start()
+
+    def start_a2(h):
+        ya(h, 2).start()
 
     def start_b(h):
         za(h).wait_recv()
@@ -137,18 +153,25 @@
     def start_c(h):
         for d in (1, 2, 3):
             yb(h, d).wait_recv()
-        for d in (1, 3, 2):
-            xc(h, d).start()
-
-    def start_e(h):
+        xc(h, 1).start()
+        xc(h, 3).start()
+
+    def start_c2(h):
+        xc(h, 2).start()
+
+    def start_e1(h):
         for d in (1, 2, 3):
             ya(h, d).wait_recv()
+        ec(h, 0).start()
+
+    def start_e2(h):
         for d in (1, 2, 3):
             xc(h, d).wait_recv()
-        ec(h).start()
+        ec(h, 1).start()
 
     def project(h):
-        ec(h).wait_recv()
+        ec(h, 0).wait_recv()
+        ec(h, 1).wait_recv()
         weight = wbuf[h].reshape(D, 2 * HD)
         result = jnp.dot(nbuf[...], weight, preferred_element_type=jnp.float32)
         kvbuf[h, 4, :, pl.ds(0, HD)] = result[:, :HD].astype(jnp.bfloat16)
@@ -203,51 +226,53 @@
             obuf[:, columns] = (output / total).astype(jnp.bfloat16)
         out_copy(h).start()
 
-    start_a(0, (1, 3))
-
-    first = s * T
-    query_pos = first + lax.broadcasted_iota(jnp.int32, (T, 1), 0)
-    begin = jnp.zeros((T, 1), jnp.int32)
-    end = dl_ref[0, 0]
-    for d in range(NDOC):
-        begin = jnp.where(query_pos >= end, end, begin)
-        if d + 1 < NDOC:
-            end = end + dl_ref[0, d + 1]
-    key_pos = first - 4 * T + lax.broadcasted_iota(jnp.int32, (T, WIN), 1)
-    bias[...] = jnp.where((key_pos <= query_pos) & (key_pos >= begin), 0.0, -jnp.inf)
-
-    start_b(0)
-    ya(0, 2).start()
-    start_a(1)
-    hid_copy.wait()
-
-    @pl.loop(0, T // 16)
+    def normalise(h):
+        hid_copy.wait()
+
+        @pl.loop(0, T // 16)
+        def _(i):
+            rows = pl.ds(pl.multiple_of(i * 16, 16), 16)
+            wide = nbuf[rows, :].astype(jnp.float32)
+            square = jnp.mean(wide * wide, axis=-1, keepdims=True)
+            nbuf[rows, :] = (wide * lax.rsqrt(square + EPS) * gain_ref[...]).astype(jnp.bfloat16)
+
+    def mask(h):
+        first = s * T
+        query_pos = first + lax.broadcasted_iota(jnp.int32, (T, 1), 0)
+        begin = jnp.zeros((T, 1), jnp.int32)
+        end = dl_ref[0, 0]
+        for d in range(NDOC):
+            begin = jnp.where(query_pos >= end, end, begin)
+            if d + 1 < NDOC:
+                end = end + dl_ref[0, d + 1]
+        key_pos = first - 4 * T + lax.broadcasted_iota(jnp.int32, (T, WIN), 1)
+        bias[...] = jnp.where((key_pos <= query_pos) & (key_pos >= begin), 0.0, -jnp.inf)
+
+    steps = {
+        "A": start_a, "A2.": start_a2, "B": start_b, "C": start_c, "C2.": start_c2,
+        "E1.": start_e1, "E2.": start_e2, "V": send_previous, "N": normalise, "M": mask,
+    }
+
+    @pl.loop(0, KVH)
     def _(i):
-        rows = pl.ds(pl.multiple_of(i * 16, 16), 16)
-        wide = nbuf[rows, :].astype(jnp.float32)
-        square = jnp.mean(wide * wide, axis=-1, keepdims=True)
-        nbuf[rows, :] = (wide * lax.rsqrt(square + EPS) * gain_ref[...]).astype(jnp.bfloat16)
+        for k in range(KVH):
+
+            @pl.when(i == k)
+            def _(k=k):
+                for word in RUNS[k]:
+                    steps[word[:-1]](int(word[-1]))
+
+        project(i)
+        send_own(i)
+
+    for word in RUNS[KVH]:
+        steps[word[:-1]](int(word[-1]))
 
     q_copy.wait()
 
-    stages = [
-        (5, send_previous),
-        (4, project),
-        (4, send_own),
-        (3, start_e),
-        (2, start_c),
-        (1, start_b),
-        (0, start_a),
-        (8, attend),
-    ]
-
-    @pl.loop(2, KVH + 8)
-    def _(i):
-        for lag, stage in stages:
-
-            @pl.when((i >= lag) & (i < KVH + lag))
-            def _(lag=lag, stage=stage):
-                stage(i - lag)
+    @pl.loop(0, KVH)
+    def _(h):
+        attend(h)
 
     @pl.loop(0, KVH)
     def _(h):
@@ -256,7 +281,8 @@
             yb(h, d).wait_send()
             xc(h, d).wait_send()
         za(h).wait_send()
-        ec(h).wait_send()
+        ec(h, 0).wait_send()
+        ec(h, 1).wait_send()
         xp(h).wait_send()
         zu(h).wait_send()
         zd(h).wait_send()

time: 151 us -> 144 us (0.954)
  Pallas kernels: 147 us -> 139 us
    pallas_call x1, Pallas kernels: 147 us -> 139 us  [shards(): pl.pallas_call(kernel, out_shape=jax.ShapeDtypeStruct((T, QH * HD), jnp.b...]
where the time goes in v3:
time: 144 us; the launch traced here: 143 us
  Pallas kernels  139 us (97%)
  local copies, waits for them, and re-layouts  3.13 us (2%)
    pallas_call x1, Pallas kernels, shards(): pl.pallas_call(kernel, out_shape=jax.ShapeDtypeStruct((T, QH * HD), jnp.b...  139 us
    unnamed x1, local copies, waits for them, and re-layouts  3.13 us

profile of v3, /device:TPU:32, one launch (start us, length us, event | category | flops | bytes accessed | tf_op | source)
XLA Modules:
  0.0 142.6 jit_solution(15112658670832956634)
XLA Ops:
  0.0 139.5 %shard_map.64 = bf16[256,4096]{1,0:T(8,128)(2,1)} custom-call(s32[1,16]{1,0:T(1,128)} %dl_ref.1, bf16[256,5120]{1,0:T(8,128)(2,1)} %bitcast.6, bf16[256,4096]{1,0:T(8,128)(2,1)} %bitcast.7, f32[1,5120]{1,0:T(1,128)} %bitcast.8, bf16[320,2048]{1,0:T(8,128)(2,1)} %w_hbm.1, f32[8,128]{1,0:T(8,128)} %bitcast.9), custom_call_target="tpu_custom_call" | custom-call | tf_op jit(solution)/shard_map/pallas_call | solution.py:297
  139.5 3.1 %copy.8 = bf16[1,256,4096]{2,1,0:T(8,128)(2,1)} copy(bf16[1,256,4096]{2,1,0:T(8,128)(2,1)} %bitcast.5) | data formatting | bytes 4194304

commit v4 on v3

--- a/solution.py
+++ b/solution.py
@@ -24,9 +24,9 @@
 
 
 RUNS = (
-    ("A0", "B0", "A1", "B1", "M0", "A2.0", "C0", "C2.0", "N0", "A2", "A2.1", "C1", "B2", "C2.1", "A3", "E1.0", "E2.0",),
-    ("C2", "A2.2", "B3", "E1.1", "E2.1", "A2.3", "C2.2", "V0",),
-    ("A4", "E1.2", "B4", "A5", "C3", "E2.2", "A6", "V1", "E1.3", "A7", "C2.3", "B5",),
+    ("A0", "B0", "A1", "B1", "M0", "A2.0", "C0", "C2.0", "A2", "N0", "A2.1", "C1", "B2", "C2.1", "A3", "A2.2", "E1.0", "E2.0",),
+    ("C2", "B3", "C2.2", "E1.1", "E2.1", "A2.3", "A4", "V0",),
+    ("E1.2", "B4", "A5", "C3", "E2.2", "A6", "V1", "E1.3", "A7", "C2.3", "B5",),
     ("A2.4", "C4", "A2.5", "E2.3", "V2", "C2.4", "B6",),
     ("C5", "E1.4", "E2.4", "B7", "C2.5", "V3",),
     ("A2.6", "C6", "E1.5", "A2.7", "E2.5", "C2.6", "E1.6", "V4",),

time: 144 us -> 143 us (level); the launches traced: 143 us -> 143 us
  no operation moved by 1% of the time
where the time goes in v4:
time: 143 us
  Pallas kernels  140 us (98%)
  local copies, waits for them, and re-layouts  3.13 us (2%)
    pallas_call x1, Pallas kernels, shards(): pl.pallas_call(kernel, out_shape=jax.ShapeDtypeStruct((T, QH * HD), jnp.b...  140 us
    unnamed x1, local copies, waits for them, and re-layouts  3.13 us

profile of v4, /device:TPU:32, one launch (start us, length us, event | category | flops | bytes accessed | tf_op | source)
XLA Modules:
  0.0 143.1 jit_solution(13181291517317071686)
XLA Ops:
  0.0 139.9 %shard_map.64 = bf16[256,4096]{1,0:T(8,128)(2,1)} custom-call(s32[1,16]{1,0:T(1,128)} %dl_ref.1, bf16[256,5120]{1,0:T(8,128)(2,1)} %bitcast.6, bf16[256,4096]{1,0:T(8,128)(2,1)} %bitcast.7, f32[1,5120]{1,0:T(1,128)} %bitcast.8, bf16[320,2048]{1,0:T(8,128)(2,1)} %w_hbm.1, f32[8,128]{1,0:T(8,128)} %bitcast.9), custom_call_target="tpu_custom_call" | custom-call | tf_op jit(solution)/shard_map/pallas_call | solution.py:297
  139.9 3.1 %copy.8 = bf16[1,256,4096]{2,1,0:T(8,128)(2,1)} copy(bf16[1,256,4096]{2,1,0:T(8,128)(2,1)} %bitcast.5) | data formatting | bytes 4194304
